TPU v7x, 32 devices: a whole 2x2x4 slice. The times are simulated.
32 devices in a mesh: groups: 2 (over x), ep: 4 (over y, core), rep: 4 (over z).
Axes of the slice: x: 2, y: 2, z: 4, core: 2. Of those that a mesh axis runs over, the one named last changes fastest.
Arguments:
- prompt_hidden: bfloat16 [8, 96, 2048], P('groups', 'ep'), parts along dimension 0, may hold values from -6 to 6
- decode_hidden: bfloat16 [64, 8, 2048], P(('groups', 'ep'), 'rep'), parts along dimension 0, may hold values from -6 to 6
- queries: bfloat16 [64, 8, 2048], P(('groups', 'ep'), None, 'rep'), parts along dimension 0, may hold values from -128 to 128
- attn_gain: float32 [2048], replicated, may hold values from 0.1 to 1.9
- key_value_weight: bfloat16 [2048, 1024], P(None, 'rep'), may hold values from -0.125 to 0.125
- out_weight: bfloat16 [2048, 2048], P('rep'), may hold values from -0.5 to 0.5
- moe_gain: float32 [2048], replicated, may hold values from 0.1 to 1.9
- gate_weight: bfloat16 [16, 2048, 768], P(('ep', 'rep')), may hold values from -0.125 to 0.125
- up_weight: bfloat16 [16, 2048, 768], P(('ep', 'rep')), may hold values from -0.125 to 0.125
- down_weight: bfloat16 [16, 768, 2048], P(('ep', 'rep')), may hold values from -0.21875 to 0.21875
- expert_table: int32 [151936], replicated, may hold values from 0 to 15, as said below
- token_ids: int32 [32, 8], P('ep', 'rep'), may hold values from 0 to 151935, as said below
- prompt_lengths: int32 [8], P('groups'), parts along dimension 0, may hold values from 1 to 96, 240 in all
Outputs:
- layer_out: bfloat16 [64, 8, 2048], P(('groups', 'ep'), 'rep'), parts along dimension 0
There are 2 independent parts, one for each index of `groups`. A program takes and returns all parts, laid end to end along the dimension named above; an argument that names none is the same for every part. Nothing has to cross between parts.
Inputs may be any that keep to these rules, and one draw needn't show every extreme that they name: `expert_table`: each expert is the value of exactly 9496 entries. `token_ids`: a device holds the 8 sequences of its index of ep at 8 // 4 steps of its index of rep; of these tokens at most 2 go to one expert; in every draw one expert receives exactly 2 from every device. `prompt_lengths`: the lengths of a group sum to 240 and the longest is 96.
All inputs are finite; a program needn't handle non-finite values.
Results may differ from a plain program's by a relative error of at most 0.017.
The roundings to bfloat16 on the way count: a program that leaves them out, or rounds other values in their place, can miss the bound.
Values may be sent and summed in bfloat16 or wider, within the bound.
No kernel may reach another device: no remote copies, remote signals or barrier semaphores. Data moves between devices by JAX's collectives and lax.ppermute only.
A program may use at most 128 MiB of HBM per device.

v0:
```python
import functools
import math

import jax
import jax.numpy as jnp
from jax import lax
from jax.experimental import pallas as pl
from jax.experimental.pallas import tpu as pltpu
from jax.sharding import PartitionSpec as P


HEAD_DIM = 128
GROUP_PROMPTS = 4
CAP = 2

EPS = 1e-06
THETA = 1000000.0


def partner(index, step, count):
    if count & (count - 1) == 0:
        return index ^ step
    return (count + step - index) % count


def swap(block, axis, step):
    count = lax.axis_size(axis)
    return lax.ppermute(block, axis, [(i, partner(i, step, count)) for i in range(count)])


def normed_of(hidden, gain_vec):
    widened = hidden.astype(jnp.float32)
    mean_sq = jnp.mean(widened * widened, axis=-1, keepdims=True)
    return (widened * lax.rsqrt(mean_sq + EPS) * gain_vec).astype(jnp.bfloat16)


def key_value(hidden, gain_vec, key_value_weight, positions, is_key):
    projected = jnp.dot(
        normed_of(hidden, gain_vec), key_value_weight, preferred_element_type=jnp.float32
    )
    half = HEAD_DIM // 2
    freq = jnp.exp(jnp.arange(half, dtype=jnp.float32) * (-2.0 * math.log(THETA) / HEAD_DIM))
    angles = positions[:, None] * freq
    cosine, sine = jnp.cos(angles), jnp.sin(angles)
    out = []
    for b in range(key_value_weight.shape[1] // HEAD_DIM):
        block = projected[:, b * HEAD_DIM : (b + 1) * HEAD_DIM]
        if is_key[b] is not False:
            first, second = block[:, :half], block[:, half:]
            turned = jnp.concatenate(
                [first * cosine - second * sine, second * cosine + first * sine], axis=1
            )
            block = turned if is_key[b] is True else jnp.where(is_key[b], turned, block)
        out.append(block.astype(jnp.bfloat16))
    return jnp.concatenate(out, axis=1) if len(out) > 1 else out[0]


def general(
    prompt_hidden,
    decode_hidden,
    queries,
    attn_gain,
    key_value_weight,
    out_weight,
    moe_gain,
    gate_weight,
    up_weight,
    down_weight,
    expert_table,
    token_ids,
    prompt_lengths,
):
    seqs, step_rows, model_width = decode_hidden.shape
    prompt_len_local = prompt_hidden.shape[1]
    qh_dev = queries.shape[2] // HEAD_DIM
    ep_count, rep_count = lax.axis_size("ep"), lax.axis_size("rep")
    ep_index, rep_index = lax.axis_index("ep"), lax.axis_index("rep")
    samples = seqs * ep_count // GROUP_PROMPTS
    blocks = key_value_weight.shape[1] // HEAD_DIM
    row_count = seqs * step_rows
    own_prompts = max(1, seqs // samples)

    own_rows = decode_hidden.reshape(row_count, model_width)
    others = [swap(own_rows, "rep", k) for k in range(1, rep_count)]
    owners = [partner(rep_index, k, rep_count) for k in range(rep_count)]

    if blocks == 1:
        is_key = [rep_index % 2 == 0]
    else:
        is_key = [b % 2 == 0 for b in range(blocks)]
    heads_here = max(1, blocks // 2)

    prompt_pos = (
        ep_index * prompt_len_local + jnp.arange(prompt_len_local, dtype=jnp.int32)
    ).astype(jnp.float32)
    prompt_part = key_value(
        prompt_hidden.reshape(-1, model_width),
        attn_gain,
        key_value_weight,
        jnp.tile(prompt_pos, GROUP_PROMPTS),
        is_key,
    ).reshape(GROUP_PROMPTS, prompt_len_local, blocks * HEAD_DIM)

    def first_prompt(ep):
        return ep * seqs // samples

    pieces, piece_pos = [], []
    for k in range(ep_count):
        other = partner(ep_index, k, ep_count)
        part = lax.dynamic_slice_in_dim(prompt_part, first_prompt(other), own_prompts, 0)
        pieces.append(swap(part, "ep", k) if k else part)
        piece_pos.append(other * prompt_len_local + jnp.arange(prompt_len_local, dtype=jnp.int32))
    prompt_kv = jnp.concatenate(pieces, axis=1)
    key_pos = jnp.concatenate(piece_pos)

    own_first = first_prompt(ep_index)
    own_lengths = lax.dynamic_slice_in_dim(prompt_lengths, own_first, own_prompts, 0)
    seq_lengths = jnp.repeat(own_lengths, seqs // own_prompts)

    def decode_part(k):
        step = owners[k] * step_rows + jnp.arange(step_rows, dtype=jnp.int32)
        position = (seq_lengths[:, None] + step[None, :]).astype(jnp.float32).reshape(-1)
        return position

    positions = [decode_part(k) for k in range(rep_count)]
    decode_own = key_value(own_rows, attn_gain, key_value_weight, positions[0], is_key)
    decode_rest = key_value(
        jnp.concatenate(others, axis=0),
        attn_gain,
        key_value_weight,
        jnp.concatenate(positions[1:]),
        is_key,
    )
    decode_kv = jnp.concatenate([decode_own, decode_rest], axis=0)
    if blocks == 1:
        partner_prompt, partner_decode = swap((prompt_kv, decode_kv), "rep", 1)
        holds_key = rep_index % 2 == 0

        def both(mine, theirs):
            return jnp.where(
                holds_key,
                jnp.concatenate([mine, theirs], axis=-1),
                jnp.concatenate([theirs, mine], axis=-1),
            )

        prompt_kv, decode_kv = both(prompt_kv, partner_prompt), both(decode_kv, partner_decode)

    tile = min(seqs // own_prompts, 8)
    tiles = seqs // own_prompts // tile
    group = qh_dev // heads_here
    by_owner = jnp.concatenate(
        [lax.dynamic_slice_in_dim(queries, o * step_rows, step_rows, 1)[None] for o in owners]
    )
    tokens = rep_count * tile * step_rows

    def tiled(rows):
        width = rows.shape[-1]
        rows = rows.reshape(rep_count, own_prompts, tiles, tile * step_rows, width)
        return rows.transpose(1, 2, 0, 3, 4).reshape(own_prompts, tiles, tokens, width)

    query_rows = tiled(by_owner.reshape(rep_count, row_count, qh_dev * HEAD_DIM))
    decode_rows = tiled(decode_kv.reshape(rep_count, row_count, -1))
    row_step = jnp.concatenate(
        [
            jnp.tile(o * step_rows + jnp.arange(step_rows, dtype=jnp.int32), tile)
            for o in owners
        ]
    )
    row_seq = jnp.tile(jnp.repeat(jnp.arange(tile, dtype=jnp.int32), step_rows), rep_count)
    self_mask = (row_seq[:, None] == row_seq[None, :]) & (row_step[None, :] <= row_step[:, None])
    prompt_mask = key_pos[None, :] < own_lengths[:, None]
    score_scale = HEAD_DIM ** (-0.5)

    heads = []
    for h in range(heads_here):
        lo = 2 * h * HEAD_DIM
        prompt_keys = prompt_kv[..., lo : lo + HEAD_DIM]
        prompt_values = prompt_kv[..., lo + HEAD_DIM : lo + 2 * HEAD_DIM]
        self_keys = decode_rows[..., lo : lo + HEAD_DIM]
        self_values = decode_rows[..., lo + HEAD_DIM : lo + 2 * HEAD_DIM]
        query = jnp.stack(
            [
                query_rows[..., (h * group + g) * HEAD_DIM : (h * group + g + 1) * HEAD_DIM]
                for g in range(group)
            ],
            axis=2,
        )
        cache_scores = score_scale * jnp.einsum(
            "pbgrd,pnd->pbgrn", query, prompt_keys, preferred_element_type=jnp.float32
        )
        self_scores = score_scale * jnp.einsum(
            "pbgrd,pbud->pbgru", query, self_keys, preferred_element_type=jnp.float32
        )
        cache_mask = prompt_mask[:, None, None, None, :]
        cache_scores = jnp.where(cache_mask, cache_scores, -1e30)
        self_scores = jnp.where(self_mask, self_scores, -1e30)
        top = jnp.maximum(
            jnp.max(cache_scores, axis=-1, keepdims=True),
            jnp.max(self_scores, axis=-1, keepdims=True),
        )
        cache_weights = jnp.where(cache_mask, jnp.exp(cache_scores - top), 0.0)
        self_weights = jnp.where(self_mask, jnp.exp(self_scores - top), 0.0)
        total = jnp.sum(cache_weights, axis=-1, keepdims=True) + jnp.sum(
            self_weights, axis=-1, keepdims=True
        )
        weighted = jnp.einsum(
            "pbgrn,pnd->pbgrd",
            cache_weights.astype(jnp.bfloat16),
            prompt_values,
            preferred_element_type=jnp.float32,
        ) + jnp.einsum(
            "pbgru,pbud->pbgrd",
            self_weights.astype(jnp.bfloat16),
            self_values,
            preferred_element_type=jnp.float32,
        )
        attended = (weighted / total).astype(jnp.bfloat16)
        heads += [attended[:, :, g] for g in range(group)]
    attended = jnp.concatenate(heads, axis=-1)
    attended = attended.reshape(own_prompts, tiles, rep_count, tile * step_rows, -1)
    attended = attended.transpose(2, 0, 1, 3, 4).reshape(rep_count * row_count, -1)

    projected = (
        jnp.dot(attended, out_weight, preferred_element_type=jnp.float32)
        .astype(jnp.bfloat16)
        .reshape(rep_count, row_count, model_width)
    )
    received = [swap(projected[k], "rep", k) for k in range(1, rep_count)]
    attn_sum = projected[0].astype(jnp.float32)
    for piece in received:
        attn_sum = attn_sum + piece.astype(jnp.float32)
    attn_mixed = (own_rows.astype(jnp.float32) + attn_sum).astype(jnp.bfloat16)

    normed = normed_of(attn_mixed, moe_gain)
    chosen = jnp.take(expert_table, token_ids.reshape(row_count))
    device_count = ep_count * rep_count
    slot_total = device_count * CAP
    same_expert = chosen[:, None] == chosen[None, :]
    before = jnp.arange(row_count)[None, :] < jnp.arange(row_count)[:, None]
    slot_rank = jnp.sum((same_expert & before).astype(jnp.int32), axis=1)
    destination = chosen * CAP + slot_rank
    send_pick = (jnp.arange(slot_total, dtype=jnp.int32)[:, None] == destination[None, :]).astype(
        jnp.bfloat16
    )
    outgoing = (
        jnp.dot(send_pick, normed, preferred_element_type=jnp.float32)
        .astype(jnp.bfloat16)
        .reshape(device_count, CAP, model_width)
    )
    arrived = lax.all_to_all(outgoing, ("ep", "rep"), split_axis=0, concat_axis=0, tiled=True)
    flat_rows = arrived.reshape(slot_total, model_width)
    gate_proj = jnp.dot(flat_rows, gate_weight[0], preferred_element_type=jnp.float32)
    up_proj = jnp.dot(flat_rows, up_weight[0], preferred_element_type=jnp.float32)
    hidden = (jax.nn.silu(gate_proj) * up_proj).astype(jnp.bfloat16)
    served = (
        jnp.dot(hidden, down_weight[0], preferred_element_type=jnp.float32)
        .astype(jnp.bfloat16)
        .reshape(device_count, CAP, model_width)
    )
    returned = lax.all_to_all(served, ("ep", "rep"), split_axis=0, concat_axis=0, tiled=True)
    moe_out = lax.dot_general(
        send_pick,
        returned.reshape(slot_total, model_width),
        (((0,), (0,)), ((), ())),
        preferred_element_type=jnp.float32,
    )
    layer_out = (attn_mixed.astype(jnp.float32) + moe_out).astype(jnp.bfloat16)
    return layer_out.reshape(seqs, step_rows, model_width)


GRANT = 16 << 20
SPAN = pl.CostEstimate(flops=1 << 32, transcendentals=0, bytes_accessed=1 << 20)
VMEM = pl.BlockSpec(memory_space=pltpu.VMEM)


def on_chip(shape, dtype):
    return pltpu.VMEM(shape, dtype)


def far(*arrays):
    return [pltpu.with_memory_space_constraint(a, pltpu.HBM) for a in arrays]


def held(*arrays):
    return [pltpu.with_memory_space_constraint(a, pltpu.VMEM) for a in arrays]


def angles_of(positions):
    half = HEAD_DIM // 2
    lane = lax.broadcasted_iota(jnp.int32, (1, HEAD_DIM), 1)
    spot = jnp.where(lane < half, lane, lane - half).astype(jnp.float32)
    angles = positions * jnp.exp(spot * (-2.0 * math.log(THETA) / HEAD_DIM))
    sine = jnp.sin(angles)
    return jnp.cos(angles), jnp.where(lane < half, -sine, sine)


def turn(block, cosine, sine):
    return block * cosine + pltpu.roll(block, HEAD_DIM // 2, 1) * sine


def column(count):
    return lax.broadcasted_iota(jnp.int32, (count, 1), 0)


HBM = pl.BlockSpec(memory_space=pltpu.HBM)


def ahead_kernel(out):
    out[...] = jnp.zeros(out.shape, out.dtype)


def ahead_part():
    return pl.pallas_call(
        ahead_kernel,
        out_shape=on_chip((8, HEAD_DIM), jnp.float32),
        out_specs=VMEM,
        compiler_params=pltpu.CompilerParams(vmem_limit_bytes=GRANT),
        cost_estimate=SPAN,
        name="ahead_part",
    )()


def prompt_kernel(seqs, samples, ahead, hidden, gain, weight, *rest):
    del ahead
    *outs, scratch = rest
    prompts, here, width = hidden.shape
    ep = lax.axis_index("ep")
    spot = lax.rem(column(prompts * here), here) + ep * here
    cosine, sine = angles_of(spot.astype(jnp.float32))
    normed = normed_of(hidden[...].astype(jnp.float32).reshape(prompts * here, width), gain[...])
    projected = jnp.dot(normed, weight[...], preferred_element_type=jnp.float32)
    keys = turn(projected[:, :HEAD_DIM], cosine, sine)
    scratch[:, :, :HEAD_DIM] = keys.reshape(prompts, here, HEAD_DIM)
    scratch[:, :, HEAD_DIM:] = projected[:, HEAD_DIM:].reshape(prompts, here, HEAD_DIM)
    for k, out in enumerate(outs):
        first = partner(ep, k, len(outs)) * seqs // samples
        out[...] = scratch[first].astype(jnp.bfloat16)


def prompt_part(ahead, prompt_hidden, gain, weight, seqs, samples, ep_count):
    prompts, here, _ = prompt_hidden.shape
    columns = weight.shape[1]
    return pl.pallas_call(
        functools.partial(prompt_kernel, seqs, samples),
        out_shape=[on_chip((here, columns), jnp.bfloat16)] * ep_count,
        in_specs=[VMEM] * 4,
        out_specs=[VMEM] * ep_count,
        scratch_shapes=[pltpu.VMEM((prompts, here, columns), jnp.float32)],
        compiler_params=pltpu.CompilerParams(vmem_limit_bytes=GRANT),
        cost_estimate=SPAN,
        name="prompt_part",
    )(ahead, prompt_hidden, gain, weight)


def place(rep, reps, own, step_rows, index):
    k = index // own
    sequence = lax.rem(index, own) // step_rows
    return partner(rep, k, reps) * step_rows + lax.rem(index, step_rows), sequence


def ready_kernel(reps, eps, here, samples, lengths, gain, weight, decode, queries, *rest):
    ordered, mask, cosine_out, sine_out, own_kv, own_rows = rest
    seqs, steps, _ = queries.shape
    step_rows = steps // reps
    own = seqs * step_rows
    total = reps * own
    ep, rep = lax.axis_index("ep"), lax.axis_index("rep")
    row_step, row_seq = place(rep, reps, own, step_rows, column(total))
    source = row_seq * steps + row_step
    pick = (source == lax.broadcasted_iota(jnp.int32, (total, total), 1)).astype(jnp.bfloat16)
    flat = queries[...].astype(jnp.float32).reshape(total, -1).astype(jnp.bfloat16)
    query = jnp.dot(pick, flat, preferred_element_type=jnp.float32).astype(jnp.bfloat16)
    for g in range(query.shape[1] // HEAD_DIM):
        ordered[g * total : (g + 1) * total, :] = query[:, g * HEAD_DIM : (g + 1) * HEAD_DIM]
    for s in range(seqs):
        own_rows[s * step_rows : (s + 1) * step_rows, :] = decode[s]
    normed = normed_of(own_rows[...], gain[...])
    projected = jnp.dot(normed, weight[...], preferred_element_type=jnp.float32)
    lane = lax.broadcasted_iota(jnp.int32, lengths.shape, 1)
    length = jnp.where(lane == ep * seqs // samples, lengths[...], 0)
    length = jnp.sum(length, axis=1, keepdims=True)
    cosine, sine = angles_of((row_step + length).astype(jnp.float32))
    cosine_out[...] = cosine[own:]
    sine_out[...] = sine[own:]
    keys = turn(projected[:, :HEAD_DIM], cosine[:own], sine[:own])
    own_kv[:, :HEAD_DIM] = keys.astype(jnp.bfloat16)
    own_kv[:, HEAD_DIM:] = projected[:, HEAD_DIM:].astype(jnp.bfloat16)
    key = lax.broadcasted_iota(jnp.int32, (1, eps * here + total), 1)
    key_ep = partner(ep, key // here, eps)
    prompt_ok = (key < eps * here) & (key_ep * here + lax.rem(key, here) < length)
    key_step, key_seq = place(rep, reps, own, step_rows, key - eps * here)
    self_ok = (key >= eps * here) & (key_seq == row_seq) & (key_step <= row_step)
    mask[...] = (prompt_ok | self_ok).astype(jnp.int32)


def ready_part(lengths, gain, weight, decode, queries, here, reps, eps, samples):
    seqs, steps, columns = queries.shape
    total, width = seqs * steps, decode.shape[2]
    own = total // reps
    return pl.pallas_call(
        functools.partial(ready_kernel, reps, eps, here, samples),
        out_shape=[
            on_chip((total * columns // HEAD_DIM, HEAD_DIM), jnp.bfloat16),
            on_chip((total, eps * here + total), jnp.int32),
            on_chip((total - own, HEAD_DIM), jnp.float32),
            on_chip((total - own, HEAD_DIM), jnp.float32),
            on_chip((own, weight.shape[1]), jnp.bfloat16),
            on_chip((own, width), jnp.bfloat16),
        ],
        in_specs=[VMEM] * 5,
        out_specs=[VMEM] * 6,
        compiler_params=pltpu.CompilerParams(vmem_limit_bytes=GRANT),
        cost_estimate=SPAN,
        name="ready_part",
    )(lengths, gain, weight, decode, queries)


def attend_kernel(reps, gain, weight, query, mask, cosine, sine, own_kv, own_rows, out_weight, *rest):
    outs, rows = rest[-reps - 1 : -1], rest[-1]
    others, prompts = rest[: reps - 1], rest[reps - 1 : -reps - 1]
    own, total = own_rows.shape[0], mask.shape[0]
    group = query.shape[0] // total
    seqs, step_rows, _ = others[0].shape
    for k, piece in enumerate(others):
        for s in range(seqs):
            at = k * own + s * step_rows
            rows[at : at + step_rows, :] = piece[s]
    normed = normed_of(rows[...], gain[...])
    projected = jnp.dot(normed, weight[...], preferred_element_type=jnp.float32)
    other_keys = turn(projected[:, :HEAD_DIM], cosine[...], sine[...]).astype(jnp.bfloat16)
    other_values = projected[:, HEAD_DIM:].astype(jnp.bfloat16)
    keys = [p[:, :HEAD_DIM] for p in prompts] + [own_kv[:, :HEAD_DIM], other_keys]
    values = [p[:, HEAD_DIM:] for p in prompts] + [own_kv[:, HEAD_DIM:], other_values]
    keys, values = jnp.concatenate(keys, axis=0), jnp.concatenate(values, axis=0)
    scores = lax.dot_general(
        query[...], keys, (((1,), (1,)), ((), ())), preferred_element_type=jnp.float32
    ) * (HEAD_DIM**-0.5)
    admitted = jnp.concatenate([mask[...]] * group, axis=0) != 0
    scores = jnp.where(admitted, scores, -1e30)
    top = jnp.max(scores, axis=1, keepdims=True)
    weights = jnp.where(admitted, jnp.exp(scores - top), 0.0)
    row_total = jnp.sum(weights, axis=1, keepdims=True)
    weighted = jnp.dot(weights.astype(jnp.bfloat16), values, preferred_element_type=jnp.float32)
    attended = (weighted / row_total).astype(jnp.bfloat16)
    attended = jnp.concatenate(
        [attended[g * total : (g + 1) * total] for g in range(group)], axis=1
    )
    projected = jnp.dot(attended, out_weight[...], preferred_element_type=jnp.float32)
    for k in range(reps):
        part = projected[k * own : (k + 1) * own]
        if k == 0:
            part = part + own_rows[...].astype(jnp.float32)
        outs[k][...] = part.astype(outs[k].dtype)


def attend_part(gain, weight, ready, others, prompts):
    own, width = ready[5].shape
    reps = 1 + len(others)
    shapes = [on_chip((own, width), jnp.float32)]
    shapes += [on_chip((own, width), jnp.bfloat16)] * (reps - 1)
    return pl.pallas_call(
        functools.partial(attend_kernel, reps),
        out_shape=shapes,
        in_specs=[VMEM] * (2 + len(ready) + len(others) + len(prompts)),
        out_specs=[VMEM] * reps,
        scratch_shapes=[pltpu.VMEM(((reps - 1) * own, width), jnp.bfloat16)],
        compiler_params=pltpu.CompilerParams(vmem_limit_bytes=GRANT),
        cost_estimate=SPAN,
        name="attend_part",
    )(gain, weight, *ready, *others, *prompts)


def route_kernel(after, ids, table, pick, pick_back, token_ids, sem):
    del after
    copy = pltpu.make_async_copy(ids, token_ids, sem)
    copy.start()
    step_rows, seqs = token_ids.shape
    count, lanes = seqs * step_rows, table.shape[1]
    lane = lax.broadcasted_iota(jnp.int32, (1, lanes), 1)
    across = jnp.full((1, count), -1, jnp.int32)
    below = jnp.full((count, 1), -1, jnp.int32)
    spot = lax.broadcasted_iota(jnp.int32, (1, count), 1)
    copy.wait()
    for i in range(count):
        token = token_ids[i % step_rows, i // step_rows]
        line = table[pl.ds(token // lanes, 1), :]
        found = jnp.sum(jnp.where(lane == lax.rem(token, lanes), line, 0), axis=1, keepdims=True)
        across = jnp.where(spot == i, found, across)
        below = jnp.where(column(count) == i, found, below)
    same = across == below
    rank = jnp.sum((same & (column(count) < spot)).astype(jnp.int32), axis=0, keepdims=True)
    rank_below = jnp.sum((same & (spot < column(count))).astype(jnp.int32), axis=1, keepdims=True)
    slots = pick.shape[0]
    pick[...] = (column(slots) == across * CAP + rank).astype(jnp.bfloat16)
    slot = lax.broadcasted_iota(jnp.int32, (1, slots), 1)
    pick_back[...] = (slot == below * CAP + rank_below).astype(jnp.bfloat16)


def route_part(after, token_ids, table, slots):
    count = token_ids.size
    token_ids, table = token_ids.T, table.reshape(-1, 128)
    return pl.pallas_call(
        route_kernel,
        out_shape=[
            on_chip((slots, count), jnp.bfloat16),
            on_chip((count, slots), jnp.bfloat16),
        ],
        in_specs=[VMEM, HBM, VMEM],
        out_specs=[VMEM] * 2,
        scratch_shapes=[pltpu.SMEM(token_ids.shape, jnp.int32), pltpu.SemaphoreType.DMA],
        compiler_params=pltpu.CompilerParams(vmem_limit_bytes=GRANT),
        cost_estimate=SPAN,
        name="route_part",
    )(after, *far(token_ids), *held(table))


def send_kernel(gain, pick, own, *rest):
    *others, mixed, outgoing = rest
    total = own[...]
    for piece in others:
        total = total + piece[...].astype(jnp.float32)
    rounded = total.astype(jnp.bfloat16)
    mixed[...] = rounded
    normed = normed_of(rounded, gain[...])
    slots = jnp.dot(pick[...], normed, preferred_element_type=jnp.float32).astype(jnp.bfloat16)
    for d in range(outgoing.shape[0]):
        outgoing[d] = slots[d * CAP : (d + 1) * CAP]


def send_part(gain, pick, shares):
    rows, width = shares[0].shape
    return pl.pallas_call(
        send_kernel,
        out_shape=[
            on_chip((rows, width), jnp.bfloat16),
            on_chip((pick.shape[0] // CAP, CAP, width), jnp.bfloat16),
        ],
        in_specs=[VMEM] * (2 + len(shares)),
        out_specs=[VMEM] * 2,
        compiler_params=pltpu.CompilerParams(vmem_limit_bytes=GRANT),
        name="send_part",
    )(gain, pick, *shares)


def expert_kernel(arrived, gate_weight, up_weight, down_weight, served, rows):
    for d in range(arrived.shape[0]):
        rows[d * CAP : (d + 1) * CAP, :] = arrived[d]
    tokens = rows[...]
    gate_proj = jnp.dot(tokens, gate_weight[0], preferred_element_type=jnp.float32)
    up_proj = jnp.dot(tokens, up_weight[0], preferred_element_type=jnp.float32)
    hidden = (gate_proj / (1.0 + jnp.exp(-gate_proj)) * up_proj).astype(jnp.bfloat16)
    result = jnp.dot(hidden, down_weight[0], preferred_element_type=jnp.float32)
    result = result.astype(jnp.bfloat16)
    for d in range(served.shape[0]):
        served[d] = result[d * CAP : (d + 1) * CAP]


def expert_part(arrived, gate_weight, up_weight, down_weight):
    return pl.pallas_call(
        expert_kernel,
        out_shape=on_chip(arrived.shape, jnp.bfloat16),
        in_specs=[VMEM] * 4,
        out_specs=VMEM,
        scratch_shapes=[pltpu.VMEM((arrived.shape[0] * CAP, arrived.shape[2]), jnp.bfloat16)],
        compiler_params=pltpu.CompilerParams(vmem_limit_bytes=GRANT),
        name="expert_part",
    )(arrived, gate_weight, up_weight, down_weight)


def final_kernel(pick_back, mixed, returned, out, rows):
    for d in range(returned.shape[0]):
        rows[d * CAP : (d + 1) * CAP, :] = returned[d]
    moe_out = jnp.dot(pick_back[...], rows[...], preferred_element_type=jnp.float32)
    total = (mixed[...].astype(jnp.float32) + moe_out).astype(jnp.bfloat16)
    step_rows = out.shape[1]
    for s in range(out.shape[0]):
        out[s] = total[s * step_rows : (s + 1) * step_rows]


def final_part(pick_back, mixed, returned, shape):
    return pl.pallas_call(
        final_kernel,
        out_shape=jax.ShapeDtypeStruct(shape, jnp.bfloat16),
        in_specs=[VMEM] * 3,
        out_specs=VMEM,
        scratch_shapes=[pltpu.VMEM((returned.shape[0] * CAP, returned.shape[2]), jnp.bfloat16)],
        compiler_params=pltpu.CompilerParams(vmem_limit_bytes=GRANT),
        name="final_part",
    )(pick_back, mixed, returned)


def local(
    prompt_hidden,
    decode_hidden,
    queries,
    attn_gain,
    key_value_weight,
    out_weight,
    moe_gain,
    gate_weight,
    up_weight,
    down_weight,
    expert_table,
    token_ids,
    prompt_lengths,
):
    seqs = decode_hidden.shape[0]
    ep_count, rep_count = lax.axis_size("ep"), lax.axis_size("rep")
    samples = seqs * ep_count // GROUP_PROMPTS
    blocks = key_value_weight.shape[1] // HEAD_DIM
    if blocks != 2 or seqs > 8 or samples % seqs or expert_table.shape[0] % 128:
        return general(
            prompt_hidden,
            decode_hidden,
            queries,
            attn_gain,
            key_value_weight,
            out_weight,
            moe_gain,
            gate_weight,
            up_weight,
            down_weight,
            expert_table,
            token_ids,
            prompt_lengths,
        )
    attn_gain, moe_gain = attn_gain[None, :], moe_gain[None, :]
    ahead = ahead_part()
    others = [swap(decode_hidden, "rep", k) for k in range(1, rep_count)]
    gain, weight, own_hidden, query = held(attn_gain, key_value_weight, decode_hidden, queries)
    parts = prompt_part(*held(ahead, prompt_hidden), gain, weight, seqs, samples, ep_count)
    prompts = [swap(part, "ep", k) if k else part for k, part in enumerate(parts)]
    ready = ready_part(
        *held(prompt_lengths[None, :]),
        gain,
        weight,
        own_hidden,
        query,
        prompt_hidden.shape[1],
        rep_count,
        ep_count,
        samples,
    )
    shares = attend_part(
        gain, weight, held(*ready, out_weight), held(*others), held(*prompts)
    )
    pick, pick_back = route_part(
        shares[0], token_ids, expert_table, ep_count * rep_count * CAP
    )
    shares = [swap(share, "rep", k) if k else share for k, share in enumerate(shares)]
    mixed, outgoing = send_part(*held(moe_gain), pick, held(*shares))
    arrived = lax.all_to_all(outgoing, ("ep", "rep"), split_axis=0, concat_axis=0, tiled=True)
    served = expert_part(*held(arrived, gate_weight, up_weight, down_weight))
    returned = lax.all_to_all(served, ("ep", "rep"), split_axis=0, concat_axis=0, tiled=True)
    return final_part(pick_back, mixed, *held(returned), decode_hidden.shape)


def solution(mesh):
    placed = (
        P("groups", "ep", None),
        P(("groups", "ep"), "rep", None),
        P(("groups", "ep"), None, "rep"),
        P(),
        P(None, "rep"),
        P("rep", None),
        P(),
        P(("ep", "rep"), None, None),
        P(("ep", "rep"), None, None),
        P(("ep", "rep"), None, None),
        P(),
        P("ep", "rep"),
        P("groups"),
    )
    return jax.shard_map(
        local,
        mesh=mesh,
        in_specs=placed,
        out_specs=P(("groups", "ep"), "rep", None),
        check_vma=False,
    )
```

profile of v0, /device:TPU:0, one launch (start us, length us, event | category | flops | bytes accessed | tf_op | source)
XLA Modules:
  0.0 49.1 jit_solution(15134850857489058905)
XLA Ops:
  0.0 0.0 copy-start.5
  0.0 0.0 copy-start.10
  0.0 0.0 copy-start.7
  0.0 1.2 %copy-done.5 = bf16[2048,256]{1,0:T(8,128)(2,1)S(1)} copy-done((bf16[2048,256]{1,0:T(8,128)(2,1)S(1)}, bf16[2048,256]{1,0:T(8,128)(2,1)}, u32[]{:S(2)}) %copy-start.5) | copy-done | bytes 1048600
  1.2 0.0 copy-done.10
  1.2 0.1 copy-done.7
  1.3 0.0 copy-start.9
  1.3 0.0 copy-start.8
  1.3 0.0 copy-start.11
  1.3 0.5 %prompt_part.1 = (bf16[24,256]{1,0:T(8,128)(2,1)S(1)}, bf16[24,256]{1,0:T(8,128)(2,1)S(1)}, bf16[24,256]{1,0:T(8,128)(2,1)S(1)}, bf16[24,256]{1,0:T(8,128)(2,1)S(1)}) custom-call(f32[8,128]{1,0:T(8,128)S(1)} %ahead_part.1.ahead, bf16[4,24,2048]{2,1,0:T(8,128)(2,1)S(1)} %copy-done.7, f32[1,2048]{1,0:T(1,128)S(1)} %bitcast.7, bf16[2048,256]{1,0:T(8,128)(2,1)S(1)} %copy-done.5), custom_call_target="tpu_custom_call" | custom-call | flops 4294967296 | bytes 1048576 | tf_op jit(solution)/shard_map/prompt_part/pallas_call | solution.py:343
  1.8 0.6 %collective-permute-start.3 = (bf16[24,256]{1,0:T(8,128)(2,1)S(1)}, bf16[24,256]{1,0:T(8,128)(2,1)S(1)}, u32[]{:S(2)}, u32[]{:S(2)}) collective-permute-start(bf16[24,256]{1,0:T(8,128)(2,1)S(1)} %get-tuple-element.30), channel_id=1, source_target_pairs={{0,4},{4,0},{8,12},{12,8},{1,5},{5,1},{9,13},{13,9},{2,6},{6,2},{1... | collective-permute-start | bytes 36872 | tf_op jit(solution)/shard_map/ppermute | solution.py:28
  2.4 0.0 copy-done.9
  2.4 2.8 %collective-permute-start = (bf16[8,2,2048]{2,1,0:T(2,128)(2,1)S(1)}, bf16[8,2,2048]{2,1,0:T(2,128)(2,1)S(1)}, u32[]{:S(2)}, u32[]{:S(2)}) collective-permute-start(bf16[8,2,2048]{2,1,0:T(2,128)(2,1)S(1)} %copy-done.9), channel_id=1, source_target_pairs={{0,1},{1,0},{2,3},{3,2},{4,5},{5,4},{6,7},{7,6},{8,9},{9,8},{10,11... | collective-permute-start | bytes 196616 | tf_op jit(solution)/shard_map/ppermute | solution.py:28
  5.2 2.5 %collective-permute-start.2 = (bf16[8,2,2048]{2,1,0:T(2,128)(2,1)S(1)}, bf16[8,2,2048]{2,1,0:T(2,128)(2,1)S(1)}, u32[]{:S(2)}, u32[]{:S(2)}) collective-permute-start(bf16[8,2,2048]{2,1,0:T(2,128)(2,1)S(1)} %copy-done.9), channel_id=1, source_target_pairs={{0,3},{1,2},{2,1},{3,0},{4,7},{5,6},{6,5},{7,4},{8,11},{9,10},{10,... | collective-permute-start | bytes 196616 | tf_op jit(solution)/shard_map/ppermute | solution.py:28
  7.7 0.1 collective-permute-start.1
  7.8 1.5 %collective-permute-start.4 = (bf16[24,256]{1,0:T(8,128)(2,1)S(1)}, bf16[24,256]{1,0:T(8,128)(2,1)S(1)}, u32[]{:S(2)}, u32[]{:S(2)}) collective-permute-start(bf16[24,256]{1,0:T(8,128)(2,1)S(1)} %get-tuple-element.31), channel_id=1, source_target_pairs={{0,8},{4,12},{8,0},{12,4},{1,9},{5,13},{9,1},{13,5},{2,10},{6,14},... | collective-permute-start | bytes 36872 | tf_op jit(solution)/shard_map/ppermute | solution.py:28
  9.3 0.0 collective-permute-done.3.rest_4_
  9.3 0.0 collective-permute-start.5
  9.3 0.0 copy-done.8
  9.3 0.0 copy-done.11
  9.4 0.0 copy-start.4
  9.4 0.4 ready_part.1
  9.8 1.7 %collective-permute-done.4.rest_5_ = bf16[24,256]{1,0:T(8,128)(2,1)S(1)} collective-permute-done((bf16[24,256]{1,0:T(8,128)(2,1)S(1)}, bf16[24,256]{1,0:T(8,128)(2,1)S(1)}, u32[]{:S(2)}, u32[]{:S(2)}) %collective-permute-start.4) | collective-permute-done | bytes 12320 | tf_op jit(solution)/shard_map/ppermute | solution.py:28
  11.5 0.9 %collective-permute-done.5.rest_6_ = bf16[24,256]{1,0:T(8,128)(2,1)S(1)} collective-permute-done((bf16[24,256]{1,0:T(8,128)(2,1)S(1)}, bf16[24,256]{1,0:T(8,128)(2,1)S(1)}, u32[]{:S(2)}, u32[]{:S(2)}) %collective-permute-start.5) | collective-permute-done | bytes 12320 | tf_op jit(solution)/shard_map/ppermute | solution.py:28
  12.5 0.0 collective-permute-done.rest_0_
  12.5 0.0 collective-permute-done.2.rest_2_
  12.5 1.8 %collective-permute-done.1.rest_1_ = bf16[8,2,2048]{2,1,0:T(2,128)(2,1)S(1)} collective-permute-done((bf16[8,2,2048]{2,1,0:T(2,128)(2,1)S(1)}, bf16[8,2,2048]{2,1,0:T(2,128)(2,1)S(1)}, u32[]{:S(2)}, u32[]{:S(2)}) %collective-permute-start.1) | collective-permute-done | bytes 65568 | tf_op jit(solution)/shard_map/ppermute | solution.py:28
  14.3 0.0 copy-done.4
  14.3 0.0 copy-start.6
  14.3 1.5 %attend_part.1 = (f32[16,2048]{1,0:T(8,128)S(1)}, bf16[16,2048]{1,0:T(8,128)(2,1)S(1)}, bf16[16,2048]{1,0:T(8,128)(2,1)S(1)}, bf16[16,2048]{1,0:T(8,128)(2,1)S(1)}) custom-call(f32[1,2048]{1,0:T(1,128)S(1)} %bitcast.9, bf16[2048,256]{1,0:T(8,128)(2,1)S(1)} %copy-done.5, bf16[256,128]{1,0:T(8,128)(2,1)S(1)} %get-tuple-element.23.query, ...), custom_call_target="tpu_custom_call" | custom-call | flops 4294967296 | bytes 1048576 | tf_op jit(solution)/shard_map/attend_part/pallas_call | solution.py:461
  15.8 0.1 collective-permute-start.6
  15.9 3.2 %collective-permute-start.7 = (bf16[16,2048]{1,0:T(8,128)(2,1)S(1)}, bf16[16,2048]{1,0:T(8,128)(2,1)S(1)}, u32[]{:S(2)}, u32[]{:S(2)}) collective-permute-start(bf16[16,2048]{1,0:T(8,128)(2,1)S(1)} %get-tuple-element.37), channel_id=1, source_target_pairs={{0,2},{1,3},{2,0},{3,1},{4,6},{5,7},{6,4},{7,5},{8,10},{9,11},{10,... | collective-permute-start | bytes 196616 | tf_op jit(solution)/shard_map/ppermute | solution.py:28
  19.1 1.1 %collective-permute-start.8 = (bf16[16,2048]{1,0:T(8,128)(2,1)S(1)}, bf16[16,2048]{1,0:T(8,128)(2,1)S(1)}, u32[]{:S(2)}, u32[]{:S(2)}) collective-permute-start(bf16[16,2048]{1,0:T(8,128)(2,1)S(1)} %get-tuple-element.38), channel_id=1, source_target_pairs={{0,3},{1,2},{2,1},{3,0},{4,7},{5,6},{6,5},{7,4},{8,11},{9,10},{10,... | collective-permute-start | bytes 196616 | tf_op jit(solution)/shard_map/ppermute | solution.py:28
  20.2 0.0 copy-done.6
  20.2 0.0 copy-start.3
  20.2 0.0 copy-start
  20.2 0.0 copy-start.1
  20.2 0.0 copy-start.2
  20.3 1.1 %route_part.1 = (bf16[32,16]{1,0:T(8,128)(2,1)S(1)}, bf16[16,32]{1,0:T(8,128)(2,1)S(1)}) custom-call(f32[16,2048]{1,0:T(8,128)S(1)} %get-tuple-element.33.after.own, s32[2,8]{1,0:T(2,128)} %bitcast.11, s32[1187,128]{1,0:T(8,128)S(1)} %bitcast.6), custom_call_target="tpu_custom_call" | custom-call | flops 4294967296 | bytes 1048576 | tf_op jit(solution)/shard_map/route_part/pallas_call | solution.py:502
  21.3 0.0 collective-permute-done.6.rest_0_
  21.3 2.4 %collective-permute-done.7.rest_1_ = bf16[16,2048]{1,0:T(8,128)(2,1)S(1)} collective-permute-done((bf16[16,2048]{1,0:T(8,128)(2,1)S(1)}, bf16[16,2048]{1,0:T(8,128)(2,1)S(1)}, u32[]{:S(2)}, u32[]{:S(2)}) %collective-permute-start.7) | collective-permute-done | bytes 65568 | tf_op jit(solution)/shard_map/ppermute | solution.py:28
  23.7 1.5 %collective-permute-done.8.rest_2_ = bf16[16,2048]{1,0:T(8,128)(2,1)S(1)} collective-permute-done((bf16[16,2048]{1,0:T(8,128)(2,1)S(1)}, bf16[16,2048]{1,0:T(8,128)(2,1)S(1)}, u32[]{:S(2)}, u32[]{:S(2)}) %collective-permute-start.8) | collective-permute-done | bytes 65568 | tf_op jit(solution)/shard_map/ppermute | solution.py:28
  25.2 0.0 copy-done.3
  25.2 0.3 send_part.1
  25.5 10.7 %all_to_all.10.arrived = bf16[16,2,2048]{2,1,0:T(2,128)(2,1)S(1)} all-to-all(bf16[16,2,2048]{2,1,0:T(2,128)(2,1)S(1)} %get-tuple-element.40), channel_id=1, replica_groups=mesh['groups'=2,'ep'=4,'rep'=4] {'ep','rep'}, dimensions={0} | all-to-all | bytes 262144 | tf_op jit(solution)/shard_map/all_to_all | solution.py:652
  36.2 0.0 copy-done
  36.2 0.0 copy-done.1
  36.2 0.0 copy-done.2
  36.2 1.7 %expert_part.1 = bf16[16,2,2048]{2,1,0:T(2,128)(2,1)S(1)} custom-call(bf16[16,2,2048]{2,1,0:T(2,128)(2,1)S(1)} %all_to_all.10.arrived, bf16[1,2048,768]{2,1,0:T(8,128)(2,1)S(1)} %copy-done, bf16[1,2048,768]{2,1,0:T(8,128)(2,1)S(1)} %copy-done.1, bf16[1,768,2048]{2,1,0:T(8,128)(2,1)S(1)} %copy-done.2), custom_call_target="tpu_custom_call" | custom-call | tf_op jit(solution)/shard_map/expert_part/pallas_call | solution.py:559
  37.9 10.3 %all_to_all.11.returned = bf16[16,2,2048]{2,1,0:T(2,128)(2,1)S(1)} all-to-all(bf16[16,2,2048]{2,1,0:T(2,128)(2,1)S(1)} %expert_part.1), channel_id=1, replica_groups=mesh['groups'=2,'ep'=4,'rep'=4] {'ep','rep'}, dimensions={0} | all-to-all | bytes 262144 | tf_op jit(solution)/shard_map/all_to_all | solution.py:654
  48.3 0.8 %final_part.1 = bf16[8,2,2048]{2,1,0:T(2,128)(2,1)} custom-call(bf16[16,32]{1,0:T(8,128)(2,1)S(1)} %get-tuple-element.34.pick_back, bf16[16,2048]{1,0:T(8,128)(2,1)S(1)} %get-tuple-element.39.mixed, bf16[16,2,2048]{2,1,0:T(2,128)(2,1)S(1)} %all_to_all.11.returned), custom_call_target="tpu_custom_call" | custom-call | tf_op jit(solution)/shard_map/final_part/pallas_call | solution.py:581
  (1 shorter events, 0.0 us)
Async XLA Ops:
  0.0 1.2 %copy-start.5 = (bf16[2048,256]{1,0:T(8,128)(2,1)S(1)}, bf16[2048,256]{1,0:T(8,128)(2,1)}, u32[]{:S(2)}) copy-start(bf16[2048,256]{1,0:T(8,128)(2,1)} %weight.5) | copy-start | bytes 3145732
  0.0 1.2 %copy-start.10 = (f32[2048]{0:T(1024)S(1)}, f32[2048]{0:T(1024)}, u32[]{:S(2)}) copy-start(f32[2048]{0:T(1024)} %param.16) | copy-start | bytes 24580
  0.0 1.3 %copy-start.7 = (bf16[4,24,2048]{2,1,0:T(8,128)(2,1)S(1)}, bf16[4,24,2048]{2,1,0:T(8,128)(2,1)}, u32[]{:S(2)}) copy-start(bf16[4,24,2048]{2,1,0:T(8,128)(2,1)} %hidden.1) | copy-start | bytes 1179652
  1.3 1.1 %copy-start.9 = (bf16[8,2,2048]{2,1,0:T(2,128)(2,1)S(1)}, bf16[8,2,2048]{2,1,0:T(2,128)(2,1)}, u32[]{:S(2)}) copy-start(bf16[8,2,2048]{2,1,0:T(2,128)(2,1)} %decode.1) | copy-start | bytes 196612
  1.3 8.0 %copy-start.8 = (bf16[8,8,512]{2,1,0:T(8,128)(2,1)S(1)}, bf16[8,8,512]{2,1,0:T(8,128)(2,1)}, u32[]{:S(2)}) copy-start(bf16[8,8,512]{2,1,0:T(8,128)(2,1)} %queries.1) | copy-start | bytes 196612
  1.3 8.0 %copy-start.11 = (s32[4]{0:T(128)S(1)}, s32[4]{0:T(128)}, u32[]{:S(2)}) copy-start(s32[4]{0:T(128)} %param.25) | copy-start | bytes 52
  1.8 7.5 %collective-permute-start.3 = (bf16[24,256]{1,0:T(8,128)(2,1)S(1)}, bf16[24,256]{1,0:T(8,128)(2,1)S(1)}, u32[]{:S(2)}, u32[]{:S(2)}) collective-permute-start(bf16[24,256]{1,0:T(8,128)(2,1)S(1)} %get-tuple-element.30), channel_id=1, source_target_pairs={{0,4},{4,0},{8,12},{12,8},{1,5},{5,1},{9,13},{13,9},{2,6},{6,2},{1... | collective-permute-start | bytes 36872 | tf_op jit(solution)/shard_map/ppermute | solution.py:28
  2.4 10.1 %collective-permute-start = (bf16[8,2,2048]{2,1,0:T(2,128)(2,1)S(1)}, bf16[8,2,2048]{2,1,0:T(2,128)(2,1)S(1)}, u32[]{:S(2)}, u32[]{:S(2)}) collective-permute-start(bf16[8,2,2048]{2,1,0:T(2,128)(2,1)S(1)} %copy-done.9), channel_id=1, source_target_pairs={{0,1},{1,0},{2,3},{3,2},{4,5},{5,4},{6,7},{7,6},{8,9},{9,8},{10,11... | collective-permute-start | bytes 196616 | tf_op jit(solution)/shard_map/ppermute | solution.py:28
  5.2 7.2 %collective-permute-start.2 = (bf16[8,2,2048]{2,1,0:T(2,128)(2,1)S(1)}, bf16[8,2,2048]{2,1,0:T(2,128)(2,1)S(1)}, u32[]{:S(2)}, u32[]{:S(2)}) collective-permute-start(bf16[8,2,2048]{2,1,0:T(2,128)(2,1)S(1)} %copy-done.9), channel_id=1, source_target_pairs={{0,3},{1,2},{2,1},{3,0},{4,7},{5,6},{6,5},{7,4},{8,11},{9,10},{10,... | collective-permute-start | bytes 196616 | tf_op jit(solution)/shard_map/ppermute | solution.py:28
  7.7 6.6 %collective-permute-start.1 = (bf16[8,2,2048]{2,1,0:T(2,128)(2,1)S(1)}, bf16[8,2,2048]{2,1,0:T(2,128)(2,1)S(1)}, u32[]{:S(2)}, u32[]{:S(2)}) collective-permute-start(bf16[8,2,2048]{2,1,0:T(2,128)(2,1)S(1)} %copy-done.9), channel_id=1, source_target_pairs={{0,2},{1,3},{2,0},{3,1},{4,6},{5,7},{6,4},{7,5},{8,10},{9,11},{10,... | collective-permute-start | bytes 196616 | tf_op jit(solution)/shard_map/ppermute | solution.py:28
  7.8 3.7 %collective-permute-start.4 = (bf16[24,256]{1,0:T(8,128)(2,1)S(1)}, bf16[24,256]{1,0:T(8,128)(2,1)S(1)}, u32[]{:S(2)}, u32[]{:S(2)}) collective-permute-start(bf16[24,256]{1,0:T(8,128)(2,1)S(1)} %get-tuple-element.31), channel_id=1, source_target_pairs={{0,8},{4,12},{8,0},{12,4},{1,9},{5,13},{9,1},{13,5},{2,10},{6,14},... | collective-permute-start | bytes 36872 | tf_op jit(solution)/shard_map/ppermute | solution.py:28
  9.3 3.1 %collective-permute-start.5 = (bf16[24,256]{1,0:T(8,128)(2,1)S(1)}, bf16[24,256]{1,0:T(8,128)(2,1)S(1)}, u32[]{:S(2)}, u32[]{:S(2)}) collective-permute-start(bf16[24,256]{1,0:T(8,128)(2,1)S(1)} %get-tuple-element.32), channel_id=1, source_target_pairs={{0,12},{4,8},{8,4},{12,0},{1,13},{5,9},{9,5},{13,1},{2,14},{6,10},... | collective-permute-start | bytes 36872 | tf_op jit(solution)/shard_map/ppermute | solution.py:28
  9.4 4.9 %copy-start.4 = (bf16[512,2048]{1,0:T(8,128)(2,1)S(1)}, bf16[512,2048]{1,0:T(8,128)(2,1)}, u32[]{:S(2)}) copy-start(bf16[512,2048]{1,0:T(8,128)(2,1)} %out_weight.1) | copy-start | bytes 6291460
  14.3 6.0 %copy-start.6 = (s32[151936]{0:T(1024)S(1)}, s32[151936]{0:T(1024)}, u32[]{:S(2)}) copy-start(s32[151936]{0:T(1024)} %param.23) | copy-start | bytes 1823236
  15.8 5.6 %collective-permute-start.6 = (bf16[16,2048]{1,0:T(8,128)(2,1)S(1)}, bf16[16,2048]{1,0:T(8,128)(2,1)S(1)}, u32[]{:S(2)}, u32[]{:S(2)}) collective-permute-start(bf16[16,2048]{1,0:T(8,128)(2,1)S(1)} %get-tuple-element.36), channel_id=1, source_target_pairs={{0,1},{1,0},{2,3},{3,2},{4,5},{5,4},{6,7},{7,6},{8,9},{9,8},{10,11... | collective-permute-start | bytes 196616 | tf_op jit(solution)/shard_map/ppermute | solution.py:28
  15.9 7.9 %collective-permute-start.7 = (bf16[16,2048]{1,0:T(8,128)(2,1)S(1)}, bf16[16,2048]{1,0:T(8,128)(2,1)S(1)}, u32[]{:S(2)}, u32[]{:S(2)}) collective-permute-start(bf16[16,2048]{1,0:T(8,128)(2,1)S(1)} %get-tuple-element.37), channel_id=1, source_target_pairs={{0,2},{1,3},{2,0},{3,1},{4,6},{5,7},{6,4},{7,5},{8,10},{9,11},{10,... | collective-permute-start | bytes 196616 | tf_op jit(solution)/shard_map/ppermute | solution.py:28
  19.1 6.1 %collective-permute-start.8 = (bf16[16,2048]{1,0:T(8,128)(2,1)S(1)}, bf16[16,2048]{1,0:T(8,128)(2,1)S(1)}, u32[]{:S(2)}, u32[]{:S(2)}) collective-permute-start(bf16[16,2048]{1,0:T(8,128)(2,1)S(1)} %get-tuple-element.38), channel_id=1, source_target_pairs={{0,3},{1,2},{2,1},{3,0},{4,7},{5,6},{6,5},{7,4},{8,11},{9,10},{10,... | collective-permute-start | bytes 196616 | tf_op jit(solution)/shard_map/ppermute | solution.py:28
  20.2 4.9 %copy-start.3 = (f32[2048]{0:T(1024)S(1)}, f32[2048]{0:T(1024)}, u32[]{:S(2)}) copy-start(f32[2048]{0:T(1024)} %param.19) | copy-start | bytes 24580
  20.2 15.9 %copy-start = (bf16[1,2048,768]{2,1,0:T(8,128)(2,1)S(1)}, bf16[1,2048,768]{2,1,0:T(8,128)(2,1)}, u32[]{:S(2)}) copy-start(bf16[1,2048,768]{2,1,0:T(8,128)(2,1)} %gate_weight.1) | copy-start | bytes 9437188
  20.2 15.9 %copy-start.1 = (bf16[1,2048,768]{2,1,0:T(8,128)(2,1)S(1)}, bf16[1,2048,768]{2,1,0:T(8,128)(2,1)}, u32[]{:S(2)}) copy-start(bf16[1,2048,768]{2,1,0:T(8,128)(2,1)} %up_weight.1) | copy-start | bytes 9437188
  20.2 15.9 %copy-start.2 = (bf16[1,768,2048]{2,1,0:T(8,128)(2,1)S(1)}, bf16[1,768,2048]{2,1,0:T(8,128)(2,1)}, u32[]{:S(2)}) copy-start(bf16[1,768,2048]{2,1,0:T(8,128)(2,1)} %down_weight.1) | copy-start | bytes 9437188
where the time goes:
time: 49.4 us; the launch traced here: 49.1 us
  blocking collectives  21 us (43%)
  starting transfers between devices  11.9 us (24%)
  waiting for transfers between devices  8.29 us (17%)
  Pallas kernels  6.4 us (13%)
  local copies, waits for them, and re-layouts  1.36 us (3%)
    ppermute x9, starting transfers between devices, swap(): lax.ppermute(block, axis, [(i, partner(i, step, count)) for i in range(co...  11.9 us
    all_to_all x1, blocking collectives, local(): lax.all_to_all(outgoing, ('ep', 'rep'), split_axis=0, concat_axis=0, tile...  10.7 us
    all_to_all x1, blocking collectives, local(): lax.all_to_all(served, ('ep', 'rep'), split_axis=0, concat_axis=0, tiled=...  10.3 us
    ppermute x9, waiting for transfers between devices, swap(): lax.ppermute(block, axis, [(i, partner(i, step, count)) for i in range(co...  8.29 us
    pallas_call x1, Pallas kernels, expert_part(): pl.pallas_call(expert_kernel, out_shape=on_chip(arrived.shape, jnp.bfloat...  1.75 us
    pallas_call x1, Pallas kernels, attend_part(): pl.pallas_call(functools.partial(attend_kernel, reps), out_shape=shapes,...  1.5 us
    unnamed x24, local copies, waits for them, and re-layouts  1.36 us
    pallas_call x1, Pallas kernels, route_part(): pl.pallas_call(route_kernel, out_shape=[on_chip((slots, count), jnp.bfloa...  1.08 us
  transfers between devices with their start and end apart: 9, of which 5 were waited for; matrix products, arithmetic and copies ran while one was open for 0% of the time, Pallas kernels for 3%

commit v1 on v0

--- a/solution.py
+++ b/solution.py
@@ -26,6 +26,12 @@
 def swap(block, axis, step):
     count = lax.axis_size(axis)
     return lax.ppermute(block, axis, [(i, partner(i, step, count)) for i in range(count)])
+
+
+def shifted(block, axis, step, sign):
+    count = lax.axis_size(axis)
+    route = [(i, (i + sign * step) % count) for i in range(count)]
+    return lax.ppermute(block, axis, route)
 
 
 def normed_of(hidden, gain_vec):
@@ -355,7 +361,7 @@
 def place(rep, reps, own, step_rows, index):
     k = index // own
     sequence = lax.rem(index, own) // step_rows
-    return partner(rep, k, reps) * step_rows + lax.rem(index, step_rows), sequence
+    return lax.rem(rep + reps - k, reps) * step_rows + lax.rem(index, step_rows), sequence
 
 
 def ready_kernel(reps, eps, here, samples, lengths, gain, weight, decode, queries, *rest):
@@ -626,7 +632,7 @@
         )
     attn_gain, moe_gain = attn_gain[None, :], moe_gain[None, :]
     ahead = ahead_part()
-    others = [swap(decode_hidden, "rep", k) for k in range(1, rep_count)]
+    others = [shifted(decode_hidden, "rep", k, 1) for k in range(1, rep_count)]
     gain, weight, own_hidden, query = held(attn_gain, key_value_weight, decode_hidden, queries)
     parts = prompt_part(*held(ahead, prompt_hidden), gain, weight, seqs, samples, ep_count)
     prompts = [swap(part, "ep", k) if k else part for k, part in enumerate(parts)]
@@ -647,7 +653,7 @@
     pick, pick_back = route_part(
         shares[0], token_ids, expert_table, ep_count * rep_count * CAP
     )
-    shares = [swap(share, "rep", k) if k else share for k, share in enumerate(shares)]
+    shares = [shifted(share, "rep", k, -1) if k else share for k, share in enumerate(shares)]
     mixed, outgoing = send_part(*held(moe_gain), pick, held(*shares))
     arrived = lax.all_to_all(outgoing, ("ep", "rep"), split_axis=0, concat_axis=0, tiled=True)
     served = expert_part(*held(arrived, gate_weight, up_weight, down_weight))

time: 49.4 us -> 49.2 us (level)
  starting transfers between devices: 11.9 us -> 11.1 us
  blocking collectives: 21 us -> 21.5 us
    ppermute x9 -> x3, starting transfers between devices: 11.9 us -> 2.08 us  [swap(): lax.ppermute(block, axis, [(i, partner(i, step, count)) for i in range(co...]
    ppermute x0 -> x6, starting transfers between devices: none -> 9.04 us  [shifted(): return lax.ppermute(block, axis, route)]
    ppermute x0 -> x6, waiting for transfers between devices: none -> 5.84 us  [shifted(): return lax.ppermute(block, axis, route)]
    ppermute x9 -> x3, waiting for transfers between devices: 8.29 us -> 2.66 us  [swap(): lax.ppermute(block, axis, [(i, partner(i, step, count)) for i in range(co...]
where the time goes in v1:
time: 49.2 us; the launch traced here: 49 us
  blocking collectives  21.5 us (44%)
  starting transfers between devices  11.1 us (23%)
  waiting for transfers between devices  8.5 us (17%)
  Pallas kernels  6.4 us (13%)
  local copies, waits for them, and re-layouts  1.36 us (3%)
    all_to_all x1, blocking collectives, local(): lax.all_to_all(outgoing, ('ep', 'rep'), split_axis=0, concat_axis=0, tile...  11.2 us
    all_to_all x1, blocking collectives, local(): lax.all_to_all(served, ('ep', 'rep'), split_axis=0, concat_axis=0, tiled=...  10.3 us
    ppermute x6, starting transfers between devices, shifted(): return lax.ppermute(block, axis, route)  9.04 us
    ppermute x6, waiting for transfers between devices, shifted(): return lax.ppermute(block, axis, route)  5.84 us
    ppermute x3, waiting for transfers between devices, swap(): lax.ppermute(block, axis, [(i, partner(i, step, count)) for i in range(co...  2.66 us
    ppermute x3, starting transfers between devices, swap(): lax.ppermute(block, axis, [(i, partner(i, step, count)) for i in range(co...  2.08 us
    pallas_call x1, Pallas kernels, expert_part(): pl.pallas_call(expert_kernel, out_shape=on_chip(arrived.shape, jnp.bfloat...  1.75 us
    pallas_call x1, Pallas kernels, attend_part(): pl.pallas_call(functools.partial(attend_kernel, reps), out_shape=shapes,...  1.49 us
  transfers between devices with their start and end apart: 9, of which 5 were waited for; matrix products, arithmetic and copies ran while one was open for 0% of the time, Pallas kernels for 3%

profile of v1, /device:TPU:0, one launch (start us, length us, event | category | flops | bytes accessed | tf_op | source)
XLA Modules:
  0.0 49.0 jit_solution(5646491803654739538)
XLA Ops:
  0.0 0.0 copy-start.5
  0.0 0.0 copy-start.10
  0.0 0.0 copy-start.7
  0.0 1.2 %copy-done.5 = bf16[2048,256]{1,0:T(8,128)(2,1)S(1)} copy-done((bf16[2048,256]{1,0:T(8,128)(2,1)S(1)}, bf16[2048,256]{1,0:T(8,128)(2,1)}, u32[]{:S(2)}) %copy-start.5) | copy-done | bytes 1048600
  1.2 0.0 copy-done.10
  1.2 0.1 copy-done.7
  1.3 0.0 copy-start.9
  1.3 0.0 copy-start.8
  1.3 0.0 copy-start.11
  1.3 0.5 %prompt_part.1 = (bf16[24,256]{1,0:T(8,128)(2,1)S(1)}, bf16[24,256]{1,0:T(8,128)(2,1)S(1)}, bf16[24,256]{1,0:T(8,128)(2,1)S(1)}, bf16[24,256]{1,0:T(8,128)(2,1)S(1)}) custom-call(f32[8,128]{1,0:T(8,128)S(1)} %ahead_part.1.ahead, bf16[4,24,2048]{2,1,0:T(8,128)(2,1)S(1)} %copy-done.7, f32[1,2048]{1,0:T(1,128)S(1)} %bitcast.7, bf16[2048,256]{1,0:T(8,128)(2,1)S(1)} %copy-done.5), custom_call_target="tpu_custom_call" | custom-call | flops 4294967296 | bytes 1048576 | tf_op jit(solution)/shard_map/prompt_part/pallas_call | solution.py:349
  1.8 0.6 %collective-permute-start.3 = (bf16[24,256]{1,0:T(8,128)(2,1)S(1)}, bf16[24,256]{1,0:T(8,128)(2,1)S(1)}, u32[]{:S(2)}, u32[]{:S(2)}) collective-permute-start(bf16[24,256]{1,0:T(8,128)(2,1)S(1)} %get-tuple-element.30), channel_id=1, source_target_pairs={{0,4},{4,0},{8,12},{12,8},{1,5},{5,1},{9,13},{13,9},{2,6},{6,2},{1... | collective-permute-start | bytes 36872 | tf_op jit(solution)/shard_map/ppermute | solution.py:28
  2.4 0.0 copy-done.9
  2.4 2.8 %collective-permute-start = (bf16[8,2,2048]{2,1,0:T(2,128)(2,1)S(1)}, bf16[8,2,2048]{2,1,0:T(2,128)(2,1)S(1)}, u32[]{:S(2)}, u32[]{:S(2)}) collective-permute-start(bf16[8,2,2048]{2,1,0:T(2,128)(2,1)S(1)} %copy-done.9), channel_id=1, source_target_pairs={{0,1},{1,2},{2,3},{3,0},{4,5},{5,6},{6,7},{7,4},{8,9},{9,10},{10,1... | collective-permute-start | bytes 196616 | tf_op jit(solution)/shard_map/ppermute | solution.py:34
  5.2 2.0 %collective-permute-start.2 = (bf16[8,2,2048]{2,1,0:T(2,128)(2,1)S(1)}, bf16[8,2,2048]{2,1,0:T(2,128)(2,1)S(1)}, u32[]{:S(2)}, u32[]{:S(2)}) collective-permute-start(bf16[8,2,2048]{2,1,0:T(2,128)(2,1)S(1)} %copy-done.9), channel_id=1, source_target_pairs={{0,3},{1,0},{2,1},{3,2},{4,7},{5,4},{6,5},{7,6},{8,11},{9,8},{10,9... | collective-permute-start | bytes 196616 | tf_op jit(solution)/shard_map/ppermute | solution.py:34
  7.2 1.0 %collective-permute-start.1 = (bf16[8,2,2048]{2,1,0:T(2,128)(2,1)S(1)}, bf16[8,2,2048]{2,1,0:T(2,128)(2,1)S(1)}, u32[]{:S(2)}, u32[]{:S(2)}) collective-permute-start(bf16[8,2,2048]{2,1,0:T(2,128)(2,1)S(1)} %copy-done.9), channel_id=1, source_target_pairs={{0,2},{1,3},{2,0},{3,1},{4,6},{5,7},{6,4},{7,5},{8,10},{9,11},{10,... | collective-permute-start | bytes 196616 | tf_op jit(solution)/shard_map/ppermute | solution.py:34
  8.3 1.5 %collective-permute-start.4 = (bf16[24,256]{1,0:T(8,128)(2,1)S(1)}, bf16[24,256]{1,0:T(8,128)(2,1)S(1)}, u32[]{:S(2)}, u32[]{:S(2)}) collective-permute-start(bf16[24,256]{1,0:T(8,128)(2,1)S(1)} %get-tuple-element.31), channel_id=1, source_target_pairs={{0,8},{4,12},{8,0},{12,4},{1,9},{5,13},{9,1},{13,5},{2,10},{6,14},... | collective-permute-start | bytes 36872 | tf_op jit(solution)/shard_map/ppermute | solution.py:28
  9.8 0.0 collective-permute-done.3.rest_4_
  9.8 0.0 collective-permute-start.5
  9.8 0.0 copy-done.8
  9.8 0.0 copy-done.11
  9.8 0.0 copy-start.4
  9.8 0.4 ready_part.1
  10.2 1.7 %collective-permute-done.4.rest_5_ = bf16[24,256]{1,0:T(8,128)(2,1)S(1)} collective-permute-done((bf16[24,256]{1,0:T(8,128)(2,1)S(1)}, bf16[24,256]{1,0:T(8,128)(2,1)S(1)}, u32[]{:S(2)}, u32[]{:S(2)}) %collective-permute-start.4) | collective-permute-done | bytes 12320 | tf_op jit(solution)/shard_map/ppermute | solution.py:28
  12.0 0.9 %collective-permute-done.5.rest_6_ = bf16[24,256]{1,0:T(8,128)(2,1)S(1)} collective-permute-done((bf16[24,256]{1,0:T(8,128)(2,1)S(1)}, bf16[24,256]{1,0:T(8,128)(2,1)S(1)}, u32[]{:S(2)}, u32[]{:S(2)}) %collective-permute-start.5) | collective-permute-done | bytes 12320 | tf_op jit(solution)/shard_map/ppermute | solution.py:28
  12.9 0.0 collective-permute-done.rest_0_
  12.9 0.0 collective-permute-done.2.rest_2_
  12.9 1.1 %collective-permute-done.1.rest_1_ = bf16[8,2,2048]{2,1,0:T(2,128)(2,1)S(1)} collective-permute-done((bf16[8,2,2048]{2,1,0:T(2,128)(2,1)S(1)}, bf16[8,2,2048]{2,1,0:T(2,128)(2,1)S(1)}, u32[]{:S(2)}, u32[]{:S(2)}) %collective-permute-start.1) | collective-permute-done | bytes 65568 | tf_op jit(solution)/shard_map/ppermute | solution.py:34
  14.0 0.0 copy-done.4
  14.0 0.0 copy-start.6
  14.0 1.5 %attend_part.1 = (f32[16,2048]{1,0:T(8,128)S(1)}, bf16[16,2048]{1,0:T(8,128)(2,1)S(1)}, bf16[16,2048]{1,0:T(8,128)(2,1)S(1)}, bf16[16,2048]{1,0:T(8,128)(2,1)S(1)}) custom-call(f32[1,2048]{1,0:T(1,128)S(1)} %bitcast.9, bf16[2048,256]{1,0:T(8,128)(2,1)S(1)} %copy-done.5, bf16[256,128]{1,0:T(8,128)(2,1)S(1)} %get-tuple-element.23.query, ...), custom_call_target="tpu_custom_call" | custom-call | flops 4294967296 | bytes 1048576 | tf_op jit(solution)/shard_map/attend_part/pallas_call | solution.py:467
  15.5 2.2 %collective-permute-start.6 = (bf16[16,2048]{1,0:T(8,128)(2,1)S(1)}, bf16[16,2048]{1,0:T(8,128)(2,1)S(1)}, u32[]{:S(2)}, u32[]{:S(2)}) collective-permute-start(bf16[16,2048]{1,0:T(8,128)(2,1)S(1)} %get-tuple-element.36), channel_id=1, source_target_pairs={{0,3},{1,0},{2,1},{3,2},{4,7},{5,4},{6,5},{7,6},{8,11},{9,8},{10,9... | collective-permute-start | bytes 196616 | tf_op jit(solution)/shard_map/ppermute | solution.py:34
  17.7 0.0 collective-permute-start.7
  17.7 1.0 %collective-permute-start.8 = (bf16[16,2048]{1,0:T(8,128)(2,1)S(1)}, bf16[16,2048]{1,0:T(8,128)(2,1)S(1)}, u32[]{:S(2)}, u32[]{:S(2)}) collective-permute-start(bf16[16,2048]{1,0:T(8,128)(2,1)S(1)} %get-tuple-element.38), channel_id=1, source_target_pairs={{0,1},{1,2},{2,3},{3,0},{4,5},{5,6},{6,7},{7,4},{8,9},{9,10},{10,1... | collective-permute-start | bytes 196616 | tf_op jit(solution)/shard_map/ppermute | solution.py:34
  18.7 0.0 copy-done.6
  18.7 0.0 copy-start.3
  18.7 0.0 copy-start
  18.7 0.0 copy-start.1
  18.7 0.0 copy-start.2
  18.7 1.1 %route_part.1 = (bf16[32,16]{1,0:T(8,128)(2,1)S(1)}, bf16[16,32]{1,0:T(8,128)(2,1)S(1)}) custom-call(f32[16,2048]{1,0:T(8,128)S(1)} %get-tuple-element.33.after.own, s32[2,8]{1,0:T(2,128)} %bitcast.11, s32[1187,128]{1,0:T(8,128)S(1)} %bitcast.6), custom_call_target="tpu_custom_call" | custom-call | flops 4294967296 | bytes 1048576 | tf_op jit(solution)/shard_map/route_part/pallas_call | solution.py:508
  19.8 0.4 collective-permute-done.6.rest_0_
  20.2 4.4 %collective-permute-done.7.rest_1_ = bf16[16,2048]{1,0:T(8,128)(2,1)S(1)} collective-permute-done((bf16[16,2048]{1,0:T(8,128)(2,1)S(1)}, bf16[16,2048]{1,0:T(8,128)(2,1)S(1)}, u32[]{:S(2)}, u32[]{:S(2)}) %collective-permute-start.7) | collective-permute-done | bytes 65568 | tf_op jit(solution)/shard_map/ppermute | solution.py:34
  24.5 0.0 collective-permute-done.8.rest_2_
  24.6 0.0 copy-done.3
  24.6 0.3 send_part.1
  24.9 11.2 %all_to_all.10.arrived = bf16[16,2,2048]{2,1,0:T(2,128)(2,1)S(1)} all-to-all(bf16[16,2,2048]{2,1,0:T(2,128)(2,1)S(1)} %get-tuple-element.40), channel_id=1, replica_groups=mesh['groups'=2,'ep'=4,'rep'=4] {'ep','rep'}, dimensions={0} | all-to-all | bytes 262144 | tf_op jit(solution)/shard_map/all_to_all | solution.py:658
  36.0 0.0 copy-done
  36.0 0.0 copy-done.1
  36.0 0.0 copy-done.2
  36.0 1.7 %expert_part.1 = bf16[16,2,2048]{2,1,0:T(2,128)(2,1)S(1)} custom-call(bf16[16,2,2048]{2,1,0:T(2,128)(2,1)S(1)} %all_to_all.10.arrived, bf16[1,2048,768]{2,1,0:T(8,128)(2,1)S(1)} %copy-done, bf16[1,2048,768]{2,1,0:T(8,128)(2,1)S(1)} %copy-done.1, bf16[1,768,2048]{2,1,0:T(8,128)(2,1)S(1)} %copy-done.2), custom_call_target="tpu_custom_call" | custom-call | tf_op jit(solution)/shard_map/expert_part/pallas_call | solution.py:565
  37.8 10.3 %all_to_all.11.returned = bf16[16,2,2048]{2,1,0:T(2,128)(2,1)S(1)} all-to-all(bf16[16,2,2048]{2,1,0:T(2,128)(2,1)S(1)} %expert_part.1), channel_id=1, replica_groups=mesh['groups'=2,'ep'=4,'rep'=4] {'ep','rep'}, dimensions={0} | all-to-all | bytes 262144 | tf_op jit(solution)/shard_map/all_to_all | solution.py:660
  48.1 0.8 %final_part.1 = bf16[8,2,2048]{2,1,0:T(2,128)(2,1)} custom-call(bf16[16,32]{1,0:T(8,128)(2,1)S(1)} %get-tuple-element.34.pick_back, bf16[16,2048]{1,0:T(8,128)(2,1)S(1)} %get-tuple-element.39.mixed, bf16[16,2,2048]{2,1,0:T(2,128)(2,1)S(1)} %all_to_all.11.returned), custom_call_target="tpu_custom_call" | custom-call | tf_op jit(solution)/shard_map/final_part/pallas_call | solution.py:587
  (1 shorter events, 0.0 us)
Async XLA Ops:
  0.0 1.2 %copy-start.5 = (bf16[2048,256]{1,0:T(8,128)(2,1)S(1)}, bf16[2048,256]{1,0:T(8,128)(2,1)}, u32[]{:S(2)}) copy-start(bf16[2048,256]{1,0:T(8,128)(2,1)} %weight.5) | copy-start | bytes 3145732
  0.0 1.2 %copy-start.10 = (f32[2048]{0:T(1024)S(1)}, f32[2048]{0:T(1024)}, u32[]{:S(2)}) copy-start(f32[2048]{0:T(1024)} %param.16) | copy-start | bytes 24580
  0.0 1.3 %copy-start.7 = (bf16[4,24,2048]{2,1,0:T(8,128)(2,1)S(1)}, bf16[4,24,2048]{2,1,0:T(8,128)(2,1)}, u32[]{:S(2)}) copy-start(bf16[4,24,2048]{2,1,0:T(8,128)(2,1)} %hidden.1) | copy-start | bytes 1179652
  1.3 1.1 %copy-start.9 = (bf16[8,2,2048]{2,1,0:T(2,128)(2,1)S(1)}, bf16[8,2,2048]{2,1,0:T(2,128)(2,1)}, u32[]{:S(2)}) copy-start(bf16[8,2,2048]{2,1,0:T(2,128)(2,1)} %decode.1) | copy-start | bytes 196612
  1.3 8.5 %copy-start.8 = (bf16[8,8,512]{2,1,0:T(8,128)(2,1)S(1)}, bf16[8,8,512]{2,1,0:T(8,128)(2,1)}, u32[]{:S(2)}) copy-start(bf16[8,8,512]{2,1,0:T(8,128)(2,1)} %queries.1) | copy-start | bytes 196612
  1.3 8.5 %copy-start.11 = (s32[4]{0:T(128)S(1)}, s32[4]{0:T(128)}, u32[]{:S(2)}) copy-start(s32[4]{0:T(128)} %param.25) | copy-start | bytes 52
  1.8 7.9 %collective-permute-start.3 = (bf16[24,256]{1,0:T(8,128)(2,1)S(1)}, bf16[24,256]{1,0:T(8,128)(2,1)S(1)}, u32[]{:S(2)}, u32[]{:S(2)}) collective-permute-start(bf16[24,256]{1,0:T(8,128)(2,1)S(1)} %get-tuple-element.30), channel_id=1, source_target_pairs={{0,4},{4,0},{8,12},{12,8},{1,5},{5,1},{9,13},{13,9},{2,6},{6,2},{1... | collective-permute-start | bytes 36872 | tf_op jit(solution)/shard_map/ppermute | solution.py:28
  2.4 10.5 %collective-permute-start = (bf16[8,2,2048]{2,1,0:T(2,128)(2,1)S(1)}, bf16[8,2,2048]{2,1,0:T(2,128)(2,1)S(1)}, u32[]{:S(2)}, u32[]{:S(2)}) collective-permute-start(bf16[8,2,2048]{2,1,0:T(2,128)(2,1)S(1)} %copy-done.9), channel_id=1, source_target_pairs={{0,1},{1,2},{2,3},{3,0},{4,5},{5,6},{6,7},{7,4},{8,9},{9,10},{10,1... | collective-permute-start | bytes 196616 | tf_op jit(solution)/shard_map/ppermute | solution.py:34
  5.2 7.7 %collective-permute-start.2 = (bf16[8,2,2048]{2,1,0:T(2,128)(2,1)S(1)}, bf16[8,2,2048]{2,1,0:T(2,128)(2,1)S(1)}, u32[]{:S(2)}, u32[]{:S(2)}) collective-permute-start(bf16[8,2,2048]{2,1,0:T(2,128)(2,1)S(1)} %copy-done.9), channel_id=1, source_target_pairs={{0,3},{1,0},{2,1},{3,2},{4,7},{5,4},{6,5},{7,6},{8,11},{9,8},{10,9... | collective-permute-start | bytes 196616 | tf_op jit(solution)/shard_map/ppermute | solution.py:34
  7.2 6.7 %collective-permute-start.1 = (bf16[8,2,2048]{2,1,0:T(2,128)(2,1)S(1)}, bf16[8,2,2048]{2,1,0:T(2,128)(2,1)S(1)}, u32[]{:S(2)}, u32[]{:S(2)}) collective-permute-start(bf16[8,2,2048]{2,1,0:T(2,128)(2,1)S(1)} %copy-done.9), channel_id=1, source_target_pairs={{0,2},{1,3},{2,0},{3,1},{4,6},{5,7},{6,4},{7,5},{8,10},{9,11},{10,... | collective-permute-start | bytes 196616 | tf_op jit(solution)/shard_map/ppermute | solution.py:34
  8.3 3.7 %collective-permute-start.4 = (bf16[24,256]{1,0:T(8,128)(2,1)S(1)}, bf16[24,256]{1,0:T(8,128)(2,1)S(1)}, u32[]{:S(2)}, u32[]{:S(2)}) collective-permute-start(bf16[24,256]{1,0:T(8,128)(2,1)S(1)} %get-tuple-element.31), channel_id=1, source_target_pairs={{0,8},{4,12},{8,0},{12,4},{1,9},{5,13},{9,1},{13,5},{2,10},{6,14},... | collective-permute-start | bytes 36872 | tf_op jit(solution)/shard_map/ppermute | solution.py:28
  9.8 3.1 %collective-permute-start.5 = (bf16[24,256]{1,0:T(8,128)(2,1)S(1)}, bf16[24,256]{1,0:T(8,128)(2,1)S(1)}, u32[]{:S(2)}, u32[]{:S(2)}) collective-permute-start(bf16[24,256]{1,0:T(8,128)(2,1)S(1)} %get-tuple-element.32), channel_id=1, source_target_pairs={{0,12},{4,8},{8,4},{12,0},{1,13},{5,9},{9,5},{13,1},{2,14},{6,10},... | collective-permute-start | bytes 36872 | tf_op jit(solution)/shard_map/ppermute | solution.py:28
  9.8 4.2 %copy-start.4 = (bf16[512,2048]{1,0:T(8,128)(2,1)S(1)}, bf16[512,2048]{1,0:T(8,128)(2,1)}, u32[]{:S(2)}) copy-start(bf16[512,2048]{1,0:T(8,128)(2,1)} %out_weight.1) | copy-start | bytes 6291460
  14.0 4.7 %copy-start.6 = (s32[151936]{0:T(1024)S(1)}, s32[151936]{0:T(1024)}, u32[]{:S(2)}) copy-start(s32[151936]{0:T(1024)} %param.23) | copy-start | bytes 1823236
  15.5 4.7 %collective-permute-start.6 = (bf16[16,2048]{1,0:T(8,128)(2,1)S(1)}, bf16[16,2048]{1,0:T(8,128)(2,1)S(1)}, u32[]{:S(2)}, u32[]{:S(2)}) collective-permute-start(bf16[16,2048]{1,0:T(8,128)(2,1)S(1)} %get-tuple-element.36), channel_id=1, source_target_pairs={{0,3},{1,0},{2,1},{3,2},{4,7},{5,4},{6,5},{7,6},{8,11},{9,8},{10,9... | collective-permute-start | bytes 196616 | tf_op jit(solution)/shard_map/ppermute | solution.py:34
  17.7 6.9 %collective-permute-start.7 = (bf16[16,2048]{1,0:T(8,128)(2,1)S(1)}, bf16[16,2048]{1,0:T(8,128)(2,1)S(1)}, u32[]{:S(2)}, u32[]{:S(2)}) collective-permute-start(bf16[16,2048]{1,0:T(8,128)(2,1)S(1)} %get-tuple-element.37), channel_id=1, source_target_pairs={{0,2},{1,3},{2,0},{3,1},{4,6},{5,7},{6,4},{7,5},{8,10},{9,11},{10,... | collective-permute-start | bytes 196616 | tf_op jit(solution)/shard_map/ppermute | solution.py:34
  17.7 6.9 %collective-permute-start.8 = (bf16[16,2048]{1,0:T(8,128)(2,1)S(1)}, bf16[16,2048]{1,0:T(8,128)(2,1)S(1)}, u32[]{:S(2)}, u32[]{:S(2)}) collective-permute-start(bf16[16,2048]{1,0:T(8,128)(2,1)S(1)} %get-tuple-element.38), channel_id=1, source_target_pairs={{0,1},{1,2},{2,3},{3,0},{4,5},{5,6},{6,7},{7,4},{8,9},{9,10},{10,1... | collective-permute-start | bytes 196616 | tf_op jit(solution)/shard_map/ppermute | solution.py:34
  18.7 5.9 %copy-start.3 = (f32[2048]{0:T(1024)S(1)}, f32[2048]{0:T(1024)}, u32[]{:S(2)}) copy-start(f32[2048]{0:T(1024)} %param.19) | copy-start | bytes 24580
  18.7 17.3 %copy-start = (bf16[1,2048,768]{2,1,0:T(8,128)(2,1)S(1)}, bf16[1,2048,768]{2,1,0:T(8,128)(2,1)}, u32[]{:S(2)}) copy-start(bf16[1,2048,768]{2,1,0:T(8,128)(2,1)} %gate_weight.1) | copy-start | bytes 9437188
  18.7 17.3 %copy-start.1 = (bf16[1,2048,768]{2,1,0:T(8,128)(2,1)S(1)}, bf16[1,2048,768]{2,1,0:T(8,128)(2,1)}, u32[]{:S(2)}) copy-start(bf16[1,2048,768]{2,1,0:T(8,128)(2,1)} %up_weight.1) | copy-start | bytes 9437188
  18.7 17.3 %copy-start.2 = (bf16[1,768,2048]{2,1,0:T(8,128)(2,1)S(1)}, bf16[1,768,2048]{2,1,0:T(8,128)(2,1)}, u32[]{:S(2)}) copy-start(bf16[1,768,2048]{2,1,0:T(8,128)(2,1)} %down_weight.1) | copy-start | bytes 9437188
